TPU v7x, 256 devices: a whole 4x4x8 slice. The times are simulated.
256 devices in a mesh: blk: 128 (over y, z, x_hi, core), mp: 2 (over x_lo).
Axes of the slice: x: 4 (x_hi: 2, x_lo: 2; x = x_hi * 2 + x_lo), y: 4, z: 8, core: 2. Of those that a mesh axis runs over, the one named last changes fastest.
Arguments:
- params: bfloat16 [128, 1024, 4096], P('blk', None, 'mp'), may hold values from -0.09375 to 0.09375
- hidden: bfloat16 [128, 384, 4096], P('blk', None, 'mp'), may hold values from -6 to 6
- targets: bfloat16 [128, 384, 1024], P('blk', None, 'mp'), may hold values from -6 to 6
Outputs:
- params_out: bfloat16 [128, 1024, 4096], P('blk', None, 'mp')
- errors: float32 [2], replicated
All inputs are finite; a program needn't handle non-finite values.
Results may differ from a plain program's by a relative error of at most 0.0085.
Values may be sent and summed in bfloat16 or wider, within the bound.
A program may use at most 128 MiB of HBM per device.

v0:
```python
import functools
import jax
import jax.numpy as jnp
from jax import lax
from jax.sharding import Mesh
from jax.sharding import PartitionSpec as P

ITERS = 2
BLK = ("blk_0", "blk_1", "blk_2", "blk_3")
BLK_MP = ("blk_0", "blk_1", "blk_2", "blk_3", "mp")
mix_third = 1.0 / 3.0
step_size = 0.1


def from_behind(block, axis, distance):
    devices = range(lax.axis_size(axis))
    route = [((i - distance) % len(devices), i) for i in devices]
    return lax.ppermute(block, axis, route)


def from_everyone(x, axis):
    copies = jnp.broadcast_to(x, (lax.axis_size(axis), *x.shape))
    return lax.all_to_all(copies, axis, split_axis=0, concat_axis=0, tiled=True)


def taken_together(x, axis):
    return from_everyone(x, axis).sum(axis=0)


def over_axes(x, axes):
    return functools.reduce(lax.psum, axes, x)


def send_tracker(track):
    track_left = from_behind(track, BLK, 1)
    track_right = from_behind(track, BLK, -1)
    return (track_left, track_right)


def on_device(params, hidden, targets):
    state = params[0]
    feats = hidden[0]
    targ_local = targets[0]
    tokens = feats.shape[0]
    hidden_total = state.shape[1] * lax.axis_size("mp")
    replicas = lax.axis_size(BLK)
    full_targ = lax.all_gather(targ_local, "mp", axis=1, tiled=True)

    def gradient(weight):
        partial_value = lax.dot_general(
            feats, weight, (((1,), (1,)), ((), ())), preferred_element_type=jnp.float32
        )
        output = taken_together(partial_value, "mp")
        resid = (output - full_targ.astype(jnp.float32)).astype(jnp.bfloat16)
        grad = lax.dot_general(
            resid, feats, (((0,), (0,)), ((), ())), preferred_element_type=jnp.float32
        )
        return grad / tokens

    older = gradient(state)
    fresh = older
    track = older.astype(jnp.bfloat16)
    track_left, track_right = send_tracker(track)
    err_list = []
    for step in range(ITERS):
        state_left = from_behind(state, BLK, 1)
        state_right = from_behind(state, BLK, -1)
        if step > 0:
            track_mix = (
                track_left.astype(jnp.float32)
                + track.astype(jnp.float32)
                + track_right.astype(jnp.float32)
            ) * mix_third
            track = (track_mix + fresh - older).astype(jnp.bfloat16)
            older = fresh
        own_state = state.astype(jnp.float32)
        diff = own_state - state_right.astype(jnp.float32)
        local_err = jnp.sum(diff * diff) / (hidden_total * replicas)
        err_list.append(local_err)
        blended = (
            state_left.astype(jnp.float32) + own_state + state_right.astype(jnp.float32)
        ) * mix_third
        new_state = (blended - step_size * track.astype(jnp.float32)).astype(jnp.bfloat16)
        if step < ITERS - 1:
            fresh = gradient(new_state)
        state = new_state
    errors = jnp.stack(err_list)
    errors = over_axes(errors, BLK_MP)
    return (state[None], errors)


def solution(mesh):
    torus = Mesh(
        mesh.devices.reshape(4, 8, 2, 2, mesh.shape["mp"]),
        ("blk_0", "blk_1", "blk_2", "blk_3", "mp"),
    )
    placed = (P(BLK, None, "mp"), P(BLK, None, "mp"), P(BLK, None, "mp"))
    return jax.shard_map(
        on_device, mesh=torus, in_specs=placed, out_specs=(P(BLK, None, "mp"), P()), check_vma=False
    )
```

profile of v0, /device:TPU:194, one launch (start us, length us, event | category | flops | bytes accessed | tf_op | source)
XLA Modules:
  0.0 420.3 jit_solution(9891182136154639013)
XLA Ops:
  0.6 0.0 copy-start
  0.6 2.1 collective-permute-start.1
  2.7 4.0 fusion.23
  6.8 2.1 broadcast_in_dim.9
  8.8 6.8 %all-to-all-start = ((f32[2,384,1024]{2,1,0:T(8,128)}), f32[2,384,1024]{2,1,0:T(8,128)}, u32[]{:S(2)}, u32[]{:S(2)}) async-start(f32[2,384,1024]{2,1,0:T(8,128)} %broadcast_in_dim.9), calls=%async_computation | async-start | bytes 6291456 | tf_op jit(solution)/shard_map/all_to_all | solution.py:23
  15.6 78.1 %all-gather = bf16[1,384,1024]{2,1,0:T(8,128)(2,1)} all-gather(bf16[1,384,512]{2,1,0:T(8,128)(2,1)S(1)} %copy-done.2), channel_id=2, replica_groups=mesh['blk_0'=4,'blk_1'=8,'blk_2'=2,'blk_3'=2,'mp'=2] {'mp'}, dimensions={2}, use_global_device_ids=true | all-gather | bytes 1179648 | tf_op jit(solution)/shard_map/all_gather | solution.py:47
  93.6 2.3 reduce_sum.36
  96.0 0.0 collective-permute-done
  96.0 13.7 %fusion.4 = (f32[]{:T(128)}, bf16[1024,2048]{1,0:T(8,128)(2,1)}, bf16[1024,2048]{1,0:T(8,128)(2,1)}, f32[1024,2048]{1,0:T(8,128)}) fusion(bf16[1024,2048]{1,0:T(8,128)(2,1)} %collective-permute-done.1, bf16[1,1024,2048]{2,1,0:T(8,128)(2,1)} %param.3, bf16[1024,2048]{1,0:T(8,128)(2,1)} %collective-permute-done, bf16[1,384,2048]{2,1,0:T(8,128)(2,1)S(1)} %copy-done, ...), kind=kOutput, calls=%fused_computation.12 | convolution fusion | flops 1643249664 | bytes 33292292 | tf_op jit(solution)/shard_map/dot_general | solution.py:55
  109.7 3.0 collective-permute-start.3
  112.7 86.1 %collective-permute-start.4 = (bf16[1024,2048]{1,0:T(8,128)(2,1)}, bf16[1024,2048]{1,0:T(8,128)(2,1)}, u32[]{:S(2)}, u32[]{:S(2)}) collective-permute-start(bf16[1024,2048]{1,0:T(8,128)(2,1)} %get-tuple-element.4), channel_id=1, source_target_pairs={{254,0},{0,2},{2,4},{4,6},{6,8},{8,10},{10,12},{12,14},{14,16},{16... | collective-permute-start | bytes 12582920 | tf_op jit(solution)/shard_map/ppermute | solution.py:18
  198.8 3.2 collective-permute-start.2
  202.1 4.0 fusion.25
  206.1 2.1 broadcast_in_dim.10
  208.2 6.6 %all-to-all-start.1 = ((f32[2,384,1024]{2,1,0:T(8,128)}), f32[2,384,1024]{2,1,0:T(8,128)}, u32[]{:S(2)}, u32[]{:S(2)}) async-start(f32[2,384,1024]{2,1,0:T(8,128)} %broadcast_in_dim.10), calls=%async_computation.1 | async-start | bytes 6291456 | tf_op jit(solution)/shard_map/all_to_all | solution.py:23
  215.4 6.3 %fusion.14 = f32[]{:T(128)} fusion(bf16[1024,2048]{1,0:T(8,128)(2,1)} %collective-permute-done.3, bf16[1024,2048]{1,0:T(8,128)(2,1)} %get-tuple-element.3), kind=kLoop, calls=%fused_computation.22 | loop fusion | flops 10485759 | bytes 8388612 | tf_op jit(solution)/shard_map/reduce_sum | solution.py:78
  222.4 0.1 pad_maximum_fusion
  222.5 10.7 %psum.35 = f32[2]{0:T(128)S(1)} all-reduce(f32[2]{0:T(128)S(1)} %pad_maximum_fusion), channel_id=1, replica_groups=mesh['blk_0'=4,'blk_1'=8,'blk_2'=2,'blk_3'=2,'mp'=2] {'blk_0'}, use_global_device_ids=true, to_apply=%region_4.0 | all-reduce | flops 2 | bytes 16 | tf_op jit(solution)/shard_map/psum | solution.py:31
  233.2 22.5 %psum.36 = f32[2]{0:T(128)S(1)} all-reduce(f32[2]{0:T(128)S(1)} %psum.35), channel_id=1, replica_groups=mesh['blk_0'=4,'blk_1'=8,'blk_2'=2,'blk_3'=2,'mp'=2] {'blk_1'}, use_global_device_ids=true, to_apply=%region_5.0 | all-reduce | flops 2 | bytes 16 | tf_op jit(solution)/shard_map/psum | solution.py:31
  255.7 138.1 %psum.37 = f32[2]{0:T(128)S(1)} all-reduce(f32[2]{0:T(128)S(1)} %psum.36), channel_id=1, replica_groups=mesh['blk_0'=4,'blk_1'=8,'blk_2'=2,'blk_3'=2,'mp'=2] {'blk_2'}, use_global_device_ids=true, to_apply=%region_6.0 | all-reduce | flops 2 | bytes 16 | tf_op jit(solution)/shard_map/psum | solution.py:31
  393.7 2.4 psum.38
  396.2 3.5 reduce_sum.37
  399.6 5.4 %psum.39 = f32[2]{0:T(128)} all-reduce(f32[2]{0:T(128)S(1)} %psum.38), channel_id=1, replica_groups=mesh['blk_0'=4,'blk_1'=8,'blk_2'=2,'blk_3'=2,'mp'=2] {'mp'}, use_global_device_ids=true, to_apply=%region_8.0 | all-reduce | flops 2 | bytes 16 | tf_op jit(solution)/shard_map/psum | solution.py:31
  405.1 15.3 %fusion.15 = bf16[1,1024,2048]{2,1,0:T(8,128)(2,1)} fusion(bf16[1024,2048]{1,0:T(8,128)(2,1)} %collective-permute-done.3, bf16[1024,2048]{1,0:T(8,128)(2,1)} %get-tuple-element.3, bf16[1024,2048]{1,0:T(8,128)(2,1)} %collective-permute-done.2, f32[1024,2048]{1,0:T(8,128)} %get-tuple-element.5, bf16[1024,2048]{1,0:T(8,128)(2,1)} %collective-permute-done.5, ...), kind=kOutput, calls=%fused_computation.24 | convolution fusion | flops 1657929728 | bytes 37486592 | tf_op jit(solution)/shard_map/dot_general | solution.py:55
  (14 shorter events, 0.0 us)
Async XLA Ops:
  0.6 2.1 copy-start
  0.6 95.3 %collective-permute-start.1 = (bf16[1024,2048]{1,0:T(8,128)(2,1)}, bf16[1024,2048]{1,0:T(8,128)(2,1)}, u32[]{:S(2)}, u32[]{:S(2)}) collective-permute-start(bf16[1024,2048]{1,0:T(8,128)(2,1)} %bitcast.37), channel_id=1, source_target_pairs={{2,0},{4,2},{6,4},{8,6},{10,8},{12,10},{14,12},{16,14},{18,16},{20... | collective-permute-start | bytes 12582920 | tf_op jit(solution)/shard_map/ppermute | solution.py:18
  2.7 93.2 %collective-permute-start = (bf16[1024,2048]{1,0:T(8,128)(2,1)}, bf16[1024,2048]{1,0:T(8,128)(2,1)}, u32[]{:S(2)}, u32[]{:S(2)}) collective-permute-start(bf16[1024,2048]{1,0:T(8,128)(2,1)} %bitcast.38), channel_id=1, source_target_pairs={{254,0},{0,2},{2,4},{4,6},{6,8},{8,10},{10,12},{12,14},{14,16},{16... | collective-permute-start | bytes 12582920 | tf_op jit(solution)/shard_map/ppermute | solution.py:18
  8.8 6.8 %copy-start.2 = (bf16[1,384,512]{2,1,0:T(8,128)(2,1)S(1)}, bf16[1,384,512]{2,1,0:T(8,128)(2,1)}, u32[]{:S(2)}) copy-start(bf16[1,384,512]{2,1,0:T(8,128)(2,1)} %param.5) | copy-start | bytes 1179652
  8.8 84.8 %all-to-all-start = ((f32[2,384,1024]{2,1,0:T(8,128)}), f32[2,384,1024]{2,1,0:T(8,128)}, u32[]{:S(2)}, u32[]{:S(2)}) async-start(f32[2,384,1024]{2,1,0:T(8,128)} %broadcast_in_dim.9), calls=%async_computation | async-start | bytes 6291456 | tf_op jit(solution)/shard_map/all_to_all | solution.py:23
  109.7 105.7 %collective-permute-start.3 = (bf16[1024,2048]{1,0:T(8,128)(2,1)}, bf16[1024,2048]{1,0:T(8,128)(2,1)}, u32[]{:S(2)}, u32[]{:S(2)}) collective-permute-start(bf16[1024,2048]{1,0:T(8,128)(2,1)} %get-tuple-element.3), channel_id=1, source_target_pairs={{2,0},{4,2},{6,4},{8,6},{10,8},{12,10},{14,12},{16,14},{18,16},{20... | collective-permute-start | bytes 12582920 | tf_op jit(solution)/shard_map/ppermute | solution.py:18
  112.7 292.4 %collective-permute-start.4 = (bf16[1024,2048]{1,0:T(8,128)(2,1)}, bf16[1024,2048]{1,0:T(8,128)(2,1)}, u32[]{:S(2)}, u32[]{:S(2)}) collective-permute-start(bf16[1024,2048]{1,0:T(8,128)(2,1)} %get-tuple-element.4), channel_id=1, source_target_pairs={{254,0},{0,2},{2,4},{4,6},{6,8},{8,10},{10,12},{12,14},{14,16},{16... | collective-permute-start | bytes 12582920 | tf_op jit(solution)/shard_map/ppermute | solution.py:18
  198.8 206.2 %collective-permute-start.5 = (bf16[1024,2048]{1,0:T(8,128)(2,1)}, bf16[1024,2048]{1,0:T(8,128)(2,1)}, u32[]{:S(2)}, u32[]{:S(2)}) collective-permute-start(bf16[1024,2048]{1,0:T(8,128)(2,1)} %get-tuple-element.4), channel_id=1, source_target_pairs={{2,0},{4,2},{6,4},{8,6},{10,8},{12,10},{14,12},{16,14},{18,16},{20... | collective-permute-start | bytes 12582920 | tf_op jit(solution)/shard_map/ppermute | solution.py:18
  198.8 206.2 %collective-permute-start.2 = (bf16[1024,2048]{1,0:T(8,128)(2,1)}, bf16[1024,2048]{1,0:T(8,128)(2,1)}, u32[]{:S(2)}, u32[]{:S(2)}) collective-permute-start(bf16[1024,2048]{1,0:T(8,128)(2,1)} %get-tuple-element.3), channel_id=1, source_target_pairs={{254,0},{0,2},{2,4},{4,6},{6,8},{8,10},{10,12},{12,14},{14,16},{16... | collective-permute-start | bytes 12582920 | tf_op jit(solution)/shard_map/ppermute | solution.py:18
  208.2 188.0 %all-to-all-start.1 = ((f32[2,384,1024]{2,1,0:T(8,128)}), f32[2,384,1024]{2,1,0:T(8,128)}, u32[]{:S(2)}, u32[]{:S(2)}) async-start(f32[2,384,1024]{2,1,0:T(8,128)} %broadcast_in_dim.10), calls=%async_computation.1 | async-start | bytes 6291456 | tf_op jit(solution)/shard_map/all_to_all | solution.py:23
  221.7 183.4 %copy-start.1 = (bf16[1,384,1024]{2,1,0:T(8,128)(2,1)S(1)}, bf16[1,384,1024]{2,1,0:T(8,128)(2,1)}, u32[]{:S(2)}) copy-start(bf16[1,384,1024]{2,1,0:T(8,128)(2,1)} %all-gather) | copy-start | bytes 2359300
where the time goes:
time: 421 us; the launch traced here: 420 us
  blocking collectives  257 us (61%)
  starting transfers between devices  108 us (26%)
  matrix products  37.1 us (9%)
  other arithmetic  12.1 us (3%)
    psum x5, blocking collectives, over_axes(): return functools.reduce(lax.psum, axes, x)  179 us
    ppermute x6, starting transfers between devices, from_behind(): return lax.ppermute(block, axis, route)  94.4 us
    all_gather x1, blocking collectives, on_device(): full_targ = lax.all_gather(targ_local, 'mp', axis=1, tiled=True)  78.1 us
    dot_general x2, matrix products, gradient(): lax.dot_general(resid, feats, (((0,), (0,)), ((), ())), preferred_element...  29 us
    all_to_all x2, starting transfers between devices, from_everyone(): return lax.all_to_all(copies, axis, split_axis=0, concat_axis=0, tiled=True)  13.3 us
  transfers between devices with their start and end apart: 8, of which 0 were waited for; matrix products, arithmetic and copies ran while one was open for 6% of the time, Pallas kernels for 0%

commit v1 on v0

--- a/solution.py
+++ b/solution.py
@@ -44,7 +44,9 @@
     tokens = feats.shape[0]
     hidden_total = state.shape[1] * lax.axis_size("mp")
     replicas = lax.axis_size(BLK)
-    full_targ = lax.all_gather(targ_local, "mp", axis=1, tiled=True)
+    full_targ = jnp.concatenate(
+        lax.all_to_all(jnp.stack([targ_local] * lax.axis_size("mp")), "mp", 0, 0), axis=1
+    )
 
     def gradient(weight):
         partial_value = lax.dot_general(

time: 421 us -> 416 us (0.988); the launches traced: 420 us -> 411 us
  blocking collectives: 257 us -> 130 us
  waiting for transfers between devices: 0.02 us -> 97.4 us
  local copies, waits for them, and re-layouts: 4.16 us -> 14.9 us
  other arithmetic: 12.1 us -> 17.3 us
  starting transfers between devices: 108 us -> 113 us
    all_to_all x2, waiting for transfers between devices: 0.01 us -> 93.7 us  [from_everyone(): return lax.all_to_all(copies, axis, split_axis=0, concat_axis=0, tiled=True)]
    all_gather x1 -> x0, blocking collectives: 78.1 us -> none  [on_device(): full_targ = lax.all_gather(targ_local, 'mp', axis=1, tiled=True)]
    psum x5, blocking collectives: 179 us -> 130 us  [over_axes(): return functools.reduce(lax.psum, axes, x)]
    reduce_sum x0 -> x2, local copies, waits for them, and re-layouts: none -> 6.1 us  [taken_together(): return from_everyone(x, axis).sum(axis=0)]
  transfers between devices with their start and end apart: 8 -> 9, of which waited for: 0 -> 3; matrix products, arithmetic and copies ran while one was open for 6% -> 10% of each run, Pallas kernels for 0% -> 0%
where the time goes in v1:
time: 416 us; the launch traced here: 411 us
  blocking collectives  130 us (31%)
  starting transfers between devices  113 us (27%)
  waiting for transfers between devices  97.4 us (23%)
  matrix products  36.2 us (9%)
  other arithmetic  17.3 us (4%)
  local copies, waits for them, and re-layouts  14.9 us (4%)
    psum x5, blocking collectives, over_axes(): return functools.reduce(lax.psum, axes, x)  130 us
    ppermute x6, starting transfers between devices, from_behind(): return lax.ppermute(block, axis, route)  95.4 us
    all_to_all x2, waiting for transfers between devices, from_everyone(): return lax.all_to_all(copies, axis, split_axis=0, concat_axis=0, tiled=True)  93.7 us
    dot_general x2, matrix products, gradient(): lax.dot_general(resid, feats, (((0,), (0,)), ((), ())), preferred_element...  26.5 us
    all_to_all x2, starting transfers between devices, from_everyone(): return lax.all_to_all(copies, axis, split_axis=0, concat_axis=0, tiled=True)  13 us
    dot_general x2, matrix products, gradient(): lax.dot_general(feats, weight, (((1,), (1,)), ((), ())), preferred_elemen...  9.7 us
  transfers between devices with their start and end apart: 9, of which 3 were waited for; matrix products, arithmetic and copies ran while one was open for 10% of the time, Pallas kernels for 0%

profile of v1, /device:TPU:194, one launch (start us, length us, event | category | flops | bytes accessed | tf_op | source)
XLA Modules:
  0.0 410.6 jit_solution(8935733535594329587)
XLA Ops:
  2.7 4.0 fusion.23
  8.8 6.8 %all-to-all-start = ((f32[2,384,1024]{2,1,0:T(8,128)}), f32[2,384,1024]{2,1,0:T(8,128)}, u32[]{:S(2)}, u32[]{:S(2)}) async-start(f32[2,384,1024]{2,1,0:T(8,128)} %broadcast_in_dim.9), calls=%async_computation | async-start | bytes 6291456 | tf_op jit(solution)/shard_map/all_to_all | solution.py:23
  16.8 68.4 %all-to-all-done = f32[2,384,1024]{2,1,0:T(8,128)} async-done(((f32[2,384,1024]{2,1,0:T(8,128)}), f32[2,384,1024]{2,1,0:T(8,128)}, u32[]{:S(2)}, u32[]{:S(2)}) %all-to-all-start) | async-done | bytes 3145760 | tf_op jit(solution)/shard_map/all_to_all | solution.py:23
  85.2 4.1 %all-to-all-start.1 = ((bf16[2,384,512]{1,2,0:T(8,128)(2,1)}), bf16[2,384,512]{1,2,0:T(8,128)(2,1)S(1)}, u32[]{:S(2)}, u32[]{:S(2)}) async-start(bf16[2,384,512]{1,2,0:T(8,128)(2,1)} %pad_maximum_fusion), calls=%async_computation.1 | async-start | bytes 1572864 | tf_op jit(solution)/shard_map/all_to_all | solution.py:48
  89.3 3.5 reduce_sum.40
  92.8 3.0 copy.9
  95.8 3.7 all-to-all-done.1
  101.1 12.1 %fusion.4 = (f32[]{:T(128)}, bf16[1024,2048]{1,0:T(8,128)(2,1)}, bf16[1024,2048]{1,0:T(8,128)(2,1)}, f32[1024,2048]{1,0:T(8,128)}) fusion(bf16[1024,2048]{1,0:T(8,128)(2,1)} %collective-permute-done.1, bf16[1,1024,2048]{2,1,0:T(8,128)(2,1)} %param.3, bf16[1024,2048]{1,0:T(8,128)(2,1)} %collective-permute-done, bf16[384,1024]{0,1:T(8,128)(2,1)S(1)} %bitcast.42, ...), kind=kOutput, calls=%fused_computation.12 | convolution fusion | flops 1642070016 | bytes 31719428 | tf_op jit(solution)/shard_map/dot_general | solution.py:57
  113.2 3.1 collective-permute-start.3
  116.3 87.0 %collective-permute-start.4 = (bf16[1024,2048]{1,0:T(8,128)(2,1)}, bf16[1024,2048]{1,0:T(8,128)(2,1)}, u32[]{:S(2)}, u32[]{:S(2)}) collective-permute-start(bf16[1024,2048]{1,0:T(8,128)(2,1)} %get-tuple-element.4), channel_id=1, source_target_pairs={{254,0},{0,2},{2,4},{4,6},{6,8},{8,10},{10,12},{12,14},{14,16},{16... | collective-permute-start | bytes 12582920 | tf_op jit(solution)/shard_map/ppermute | solution.py:18
  203.3 3.2 collective-permute-start.2
  206.5 5.7 %fusion.25 = f32[384,1024]{0,1:T(8,128)} fusion(bf16[1024,2048]{1,0:T(8,128)(2,1)} %get-tuple-element.3, bf16[1,384,2048]{2,1,0:T(8,128)(2,1)S(1)} %copy-done), kind=kOutput, calls=%fused_computation.36 | convolution fusion | flops 1610612736 | bytes 7340032 | tf_op jit(solution)/shard_map/dot_general | solution.py:52
  212.2 3.1 copy.12
  215.3 3.5 broadcast_in_dim.10
  218.8 6.3 %all-to-all-start.2 = ((f32[2,384,1024]{2,1,0:T(8,128)}), f32[2,384,1024]{2,1,0:T(8,128)}, u32[]{:S(2)}, u32[]{:S(2)}) async-start(f32[2,384,1024]{2,1,0:T(8,128)} %broadcast_in_dim.10), calls=%async_computation.2 | async-start | bytes 6291456 | tf_op jit(solution)/shard_map/all_to_all | solution.py:23
  225.7 6.3 %fusion.14 = f32[]{:T(128)} fusion(bf16[1024,2048]{1,0:T(8,128)(2,1)} %collective-permute-done.3, bf16[1024,2048]{1,0:T(8,128)(2,1)} %get-tuple-element.3), kind=kLoop, calls=%fused_computation.22 | loop fusion | flops 10485759 | bytes 8388612 | tf_op jit(solution)/shard_map/reduce_sum | solution.py:80
  232.7 10.7 %psum.35 = f32[2]{0:T(128)S(1)} all-reduce(f32[2]{0:T(128)S(1)} %pad_maximum_fusion.1), channel_id=1, replica_groups=mesh['blk_0'=4,'blk_1'=8,'blk_2'=2,'blk_3'=2,'mp'=2] {'blk_0'}, use_global_device_ids=true, to_apply=%region_4.0 | all-reduce | flops 2 | bytes 16 | tf_op jit(solution)/shard_map/psum | solution.py:31
  243.4 16.7 %psum.36 = f32[2]{0:T(128)S(1)} all-reduce(f32[2]{0:T(128)S(1)} %psum.35), channel_id=1, replica_groups=mesh['blk_0'=4,'blk_1'=8,'blk_2'=2,'blk_3'=2,'mp'=2] {'blk_1'}, use_global_device_ids=true, to_apply=%region_5.0 | all-reduce | flops 2 | bytes 16 | tf_op jit(solution)/shard_map/psum | solution.py:31
  260.1 25.3 %all-to-all-done.2 = f32[2,384,1024]{2,1,0:T(8,128)} async-done(((f32[2,384,1024]{2,1,0:T(8,128)}), f32[2,384,1024]{2,1,0:T(8,128)}, u32[]{:S(2)}, u32[]{:S(2)}) %all-to-all-start.2) | async-done | bytes 3145760 | tf_op jit(solution)/shard_map/all_to_all | solution.py:23
  285.4 3.5 reduce_sum.42
  288.8 94.7 %psum.37 = f32[2]{0:T(128)S(1)} all-reduce(f32[2]{0:T(128)S(1)} %psum.36), channel_id=1, replica_groups=mesh['blk_0'=4,'blk_1'=8,'blk_2'=2,'blk_3'=2,'mp'=2] {'blk_2'}, use_global_device_ids=true, to_apply=%region_6.0 | all-reduce | flops 2 | bytes 16 | tf_op jit(solution)/shard_map/psum | solution.py:31
  383.6 3.1 copy.13
  390.6 5.6 %psum.39 = f32[2]{0:T(128)} all-reduce(f32[2]{0:T(128)S(1)} %psum.38), channel_id=1, replica_groups=mesh['blk_0'=4,'blk_1'=8,'blk_2'=2,'blk_3'=2,'mp'=2] {'mp'}, use_global_device_ids=true, to_apply=%region_8.0 | all-reduce | flops 2 | bytes 16 | tf_op jit(solution)/shard_map/psum | solution.py:31
  396.3 14.4 %fusion.15 = bf16[1,1024,2048]{2,1,0:T(8,128)(2,1)} fusion(bf16[1024,2048]{1,0:T(8,128)(2,1)} %collective-permute-done.3, bf16[1024,2048]{1,0:T(8,128)(2,1)} %get-tuple-element.3, bf16[1024,2048]{1,0:T(8,128)(2,1)} %collective-permute-done.2, f32[1024,2048]{1,0:T(8,128)} %get-tuple-element.5, bf16[384,1024]{0,1:T(8,128)(2,1)S(1)} %bitcast.43, ...), kind=kOutput, calls=%fused_computation.24 | convolution fusion | flops 1656750080 | bytes 35913728 | tf_op jit(solution)/shard_map/dot_general | solution.py:57
  (20 shorter events, 11.0 us)
Async XLA Ops:
  0.6 2.1 copy-start
  0.6 100.4 %collective-permute-start.1 = (bf16[1024,2048]{1,0:T(8,128)(2,1)}, bf16[1024,2048]{1,0:T(8,128)(2,1)}, u32[]{:S(2)}, u32[]{:S(2)}) collective-permute-start(bf16[1024,2048]{1,0:T(8,128)(2,1)} %bitcast.40), channel_id=1, source_target_pairs={{2,0},{4,2},{6,4},{8,6},{10,8},{12,10},{14,12},{16,14},{18,16},{20... | collective-permute-start | bytes 12582920 | tf_op jit(solution)/shard_map/ppermute | solution.py:18
  2.7 98.4 %collective-permute-start = (bf16[1024,2048]{1,0:T(8,128)(2,1)}, bf16[1024,2048]{1,0:T(8,128)(2,1)}, u32[]{:S(2)}, u32[]{:S(2)}) collective-permute-start(bf16[1024,2048]{1,0:T(8,128)(2,1)} %bitcast.41), channel_id=1, source_target_pairs={{254,0},{0,2},{2,4},{4,6},{6,8},{8,10},{10,12},{12,14},{14,16},{16... | collective-permute-start | bytes 12582920 | tf_op jit(solution)/shard_map/ppermute | solution.py:18
  8.8 6.8 %copy-start.1 = (bf16[1,384,512]{2,1,0:T(8,128)(2,1)S(1)}, bf16[1,384,512]{2,1,0:T(8,128)(2,1)}, u32[]{:S(2)}) copy-start(bf16[1,384,512]{2,1,0:T(8,128)(2,1)} %param.5) | copy-start | bytes 1179652
  8.8 76.4 %all-to-all-start = ((f32[2,384,1024]{2,1,0:T(8,128)}), f32[2,384,1024]{2,1,0:T(8,128)}, u32[]{:S(2)}, u32[]{:S(2)}) async-start(f32[2,384,1024]{2,1,0:T(8,128)} %broadcast_in_dim.9), calls=%async_computation | async-start | bytes 6291456 | tf_op jit(solution)/shard_map/all_to_all | solution.py:23
  85.2 14.3 %all-to-all-start.1 = ((bf16[2,384,512]{1,2,0:T(8,128)(2,1)}), bf16[2,384,512]{1,2,0:T(8,128)(2,1)S(1)}, u32[]{:S(2)}, u32[]{:S(2)}) async-start(bf16[2,384,512]{1,2,0:T(8,128)(2,1)} %pad_maximum_fusion), calls=%async_computation.1 | async-start | bytes 1572864 | tf_op jit(solution)/shard_map/all_to_all | solution.py:48
  113.2 112.5 %collective-permute-start.3 = (bf16[1024,2048]{1,0:T(8,128)(2,1)}, bf16[1024,2048]{1,0:T(8,128)(2,1)}, u32[]{:S(2)}, u32[]{:S(2)}) collective-permute-start(bf16[1024,2048]{1,0:T(8,128)(2,1)} %get-tuple-element.3), channel_id=1, source_target_pairs={{2,0},{4,2},{6,4},{8,6},{10,8},{12,10},{14,12},{16,14},{18,16},{20... | collective-permute-start | bytes 12582920 | tf_op jit(solution)/shard_map/ppermute | solution.py:18
  116.3 279.9 %collective-permute-start.4 = (bf16[1024,2048]{1,0:T(8,128)(2,1)}, bf16[1024,2048]{1,0:T(8,128)(2,1)}, u32[]{:S(2)}, u32[]{:S(2)}) collective-permute-start(bf16[1024,2048]{1,0:T(8,128)(2,1)} %get-tuple-element.4), channel_id=1, source_target_pairs={{254,0},{0,2},{2,4},{4,6},{6,8},{8,10},{10,12},{12,14},{14,16},{16... | collective-permute-start | bytes 12582920 | tf_op jit(solution)/shard_map/ppermute | solution.py:18
  203.3 193.0 %collective-permute-start.5 = (bf16[1024,2048]{1,0:T(8,128)(2,1)}, bf16[1024,2048]{1,0:T(8,128)(2,1)}, u32[]{:S(2)}, u32[]{:S(2)}) collective-permute-start(bf16[1024,2048]{1,0:T(8,128)(2,1)} %get-tuple-element.4), channel_id=1, source_target_pairs={{2,0},{4,2},{6,4},{8,6},{10,8},{12,10},{14,12},{16,14},{18,16},{20... | collective-permute-start | bytes 12582920 | tf_op jit(solution)/shard_map/ppermute | solution.py:18
  203.3 193.0 %collective-permute-start.2 = (bf16[1024,2048]{1,0:T(8,128)(2,1)}, bf16[1024,2048]{1,0:T(8,128)(2,1)}, u32[]{:S(2)}, u32[]{:S(2)}) collective-permute-start(bf16[1024,2048]{1,0:T(8,128)(2,1)} %get-tuple-element.3), channel_id=1, source_target_pairs={{254,0},{0,2},{2,4},{4,6},{6,8},{8,10},{10,12},{12,14},{14,16},{16... | collective-permute-start | bytes 12582920 | tf_op jit(solution)/shard_map/ppermute | solution.py:18
  218.8 66.6 %all-to-all-start.2 = ((f32[2,384,1024]{2,1,0:T(8,128)}), f32[2,384,1024]{2,1,0:T(8,128)}, u32[]{:S(2)}, u32[]{:S(2)}) async-start(f32[2,384,1024]{2,1,0:T(8,128)} %broadcast_in_dim.10), calls=%async_computation.2 | async-start | bytes 6291456 | tf_op jit(solution)/shard_map/all_to_all | solution.py:23
